TPU v7x, 32 devices: a whole 2x2x4 slice. The times are simulated.
32 devices in a mesh: seq: 8 (over z, y), head: 4 (over x, core).
Axes of the slice: x: 2, y: 2, z: 4, core: 2. Of those that a mesh axis runs over, the one named last changes fastest.
Arguments:
- queries: bfloat16 [4096, 2048], P('seq', 'head'), may hold values from -6 to 6
- keys: bfloat16 [4096, 2048], P('seq', 'head'), may hold values from -6 to 6
- values: bfloat16 [4096, 4096], P('seq', 'head'), may hold values from -6 to 6
- forget_gate: float32 [4096, 8], P('seq', 'head'), may hold values from -1 to 14
- input_gate: float32 [4096, 8], P('seq', 'head'), may hold values from -5 to 215
- out_weight: bfloat16 [4096, 4096], P('head'), may hold values from -0.125 to 0.125
Outputs:
- mixed: bfloat16 [4096, 4096], P('seq', 'head')
- gate_mean: float32 [8], P('head')
All inputs are finite; a program needn't handle non-finite values.
Results may differ from a plain program's by a relative error of at most 0.01.
Values may be sent and summed in bfloat16 or wider, within the bound.
A program may use at most 192 MiB of HBM per device.

v0:
```python
import math

import jax
import jax.numpy as jnp
from jax import lax
from jax.sharding import PartitionSpec as P


def entering(part, axis, combine, identity):
    place = lax.axis_index(axis)
    gathered = jax.tree.map(lambda a: lax.all_gather(a, axis), part)
    state = jax.tree.map(lambda a, e: jnp.zeros_like(a) + jnp.asarray(e, a.dtype), part, identity)

    def one(lap, state):
        return combine(
            state, jax.tree.map(lambda a: lax.dynamic_index_in_dim(a, lap, 0, False), gathered)
        )

    return lax.fori_loop(0, place, one, state)


def combine_states(earlier, later_state):
    e_matrix, e_norm, e_max, e_decay = earlier
    l_matrix, l_norm, l_max, l_decay = later_state
    merged_max = jnp.maximum(l_decay + e_max, l_max)
    e_scale = jnp.exp(l_decay + e_max - merged_max)
    l_scale = jnp.exp(l_max - merged_max)
    return (
        e_scale[:, None, None] * e_matrix + l_scale[:, None, None] * l_matrix,
        e_scale[:, None] * e_norm + l_scale[:, None] * l_norm,
        merged_max,
        e_decay + l_decay,
    )


def intra_terms(q_heads, k_heads, v_heads, cum_decay, input_block):
    length = q_heads.shape[0]
    positions = jnp.arange(length)
    causal = positions[:, None] >= positions[None, :]
    log_weight = cum_decay.T[:, :, None] - cum_decay.T[:, None, :] + input_block.T[:, None, :]
    log_weight = jnp.where(causal[None], log_weight, -jnp.inf)
    intra_max = jnp.max(log_weight, axis=2)
    factors = jnp.exp(log_weight - intra_max[:, :, None])
    scores = jnp.einsum(
        "thd,shd->hts", q_heads, k_heads, preferred_element_type=jnp.float32
    ) / math.sqrt(q_heads.shape[2])
    weighted = factors * scores
    intra_den = jnp.sum(weighted, axis=2)
    rounded_weights = weighted.astype(jnp.bfloat16)
    intra_num = jnp.einsum(
        "hts,shv->thv", rounded_weights, v_heads, preferred_element_type=jnp.float32
    )
    return (intra_num, intra_den, intra_max)


def own_terms(k_heads, v_heads, cum_decay, input_block):
    block_decay = cum_decay[-1]
    own_log = block_decay[None, :] - cum_decay + input_block
    own_max = jnp.max(own_log, axis=0)
    key_weight = jnp.exp(own_log - own_max[None, :]) / math.sqrt(k_heads.shape[2])
    weighted_keys = k_heads.astype(jnp.float32) * key_weight[:, :, None]
    own_norm = jnp.sum(weighted_keys, axis=0)
    rounded_keys = weighted_keys.astype(jnp.bfloat16)
    own_matrix = jnp.einsum(
        "shv,shk->hvk", v_heads, rounded_keys, preferred_element_type=jnp.float32
    )
    return (own_matrix, own_norm, own_max, block_decay)


def readout(intra, carried_state, q_heads, cum_decay):
    intra_num, intra_den, intra_max = intra
    carry_matrix, carry_norm, carry_max, unused_decay = carried_state
    carried_log = cum_decay.T + carry_max[:, None]
    stabilizer = jnp.maximum(intra_max, carried_log)
    intra_scale = jnp.exp(intra_max - stabilizer).T
    carry_scale = jnp.exp(carried_log - stabilizer).T
    q_float = q_heads.astype(jnp.float32)
    carried_num = jnp.einsum("hvk,thk->thv", carry_matrix, q_float, precision=lax.Precision.HIGHEST)
    carried_den = jnp.einsum("hk,thk->th", carry_norm, q_float, precision=lax.Precision.HIGHEST)
    numerator = intra_scale[:, :, None] * intra_num + carry_scale[:, :, None] * carried_num
    denominator = intra_scale * intra_den.T + carry_scale * carried_den
    return (numerator / jnp.maximum(jnp.abs(denominator), 1.0)[:, :, None]).astype(jnp.bfloat16)


def shards(queries, keys, values, forget_gate, input_gate, out_weight):
    token_count = queries.shape[0]
    head_count = forget_gate.shape[1]
    qk_width = queries.shape[1] // head_count
    v_width = values.shape[1] // head_count
    q_heads = queries.reshape(token_count, head_count, qk_width)
    k_heads = keys.reshape(token_count, head_count, qk_width)
    v_heads = values.reshape(token_count, head_count, v_width)
    cum_decay = jnp.cumsum(jax.nn.log_sigmoid(forget_gate), axis=0)
    own_state = own_terms(k_heads, v_heads, cum_decay, input_gate)
    identity = (
        jnp.zeros((head_count, v_width, qk_width), jnp.float32),
        jnp.zeros((head_count, qk_width), jnp.float32),
        jnp.full((head_count,), -1e30, jnp.float32),
        jnp.zeros((head_count,), jnp.float32),
    )
    carried_state = entering(own_state, "seq", combine_states, identity)
    intra = intra_terms(q_heads, k_heads, v_heads, cum_decay, input_gate)
    hidden = readout(intra, carried_state, q_heads, cum_decay).reshape(
        token_count, head_count * v_width
    )
    partial_value = jnp.dot(hidden, out_weight, preferred_element_type=jnp.float32)
    mixed = lax.psum_scatter(
        partial_value.astype(jnp.bfloat16), "head", scatter_dimension=1, tiled=True
    )
    gate_total = lax.psum(jnp.sum(input_gate, axis=0), "seq")
    gate_mean = gate_total / (token_count * lax.axis_size("seq"))
    return (mixed, gate_mean)


def solution(mesh):
    placed = (
        P("seq", "head"),
        P("seq", "head"),
        P("seq", "head"),
        P("seq", "head"),
        P("seq", "head"),
        P("head", None),
    )
    return jax.shard_map(
        shards, mesh=mesh, in_specs=placed, out_specs=(P("seq", "head"), P("head")), check_vma=False
    )
```

profile of v0, /device:TPU:25, one launch (start us, length us, event | category | flops | bytes accessed | tf_op | source)
XLA Modules:
  0.0 214.5 jit_solution(17750209250454976476)
XLA Ops:
  7.2 0.8 fusion.18
  8.0 0.6 reduce-window.6
  9.2 1.5 copy.48
  11.8 1.3 copy.33
  13.1 12.2 %all-gather.2 = f32[8,1,2]{2,1,0:T(1,128)S(1)} all-gather(f32[1,1,2]{2,1,0:T(1,128)S(1)} %bitcast.128), channel_id=1, replica_groups=mesh['seq'=8,'head'=4] {'seq'}, dimensions={0}, use_global_device_ids=true | all-gather | bytes 72 | tf_op jit(solution)/shard_map/all_gather | solution.py:11
  25.4 0.6 dynamic-slice
  26.9 16.3 %all-reduce.1 = (f32[16]{0:T(128)S(1)}, f32[2]{0:T(128)S(1)}) all-reduce(f32[16]{0:T(128)S(1)} %dynamic-update-slice, f32[2]{0:T(128)S(1)} %get-tuple-element.133), channel_id=2, replica_groups=mesh['seq'=8,'head'=4] {'seq'}, use_global_device_ids=true, to_apply=%add | all-reduce | flops 18 | bytes 144
  43.7 1.3 multiply_reduce_fusion
  45.0 1.3 copy.49
  46.3 22.3 %all_gather.24 = f32[8,2,256]{2,1,0:T(2,128)S(1)} all-gather(f32[1,2,256]{2,1,0:T(2,128)S(1)} %all_gather.23), channel_id=1, replica_groups=mesh['seq'=8,'head'=4] {'seq'}, dimensions={0}, use_global_device_ids=true | all-gather | bytes 18432 | tf_op jit(solution)/shard_map/all_gather | solution.py:11
  69.0 1.1 fusion.29
  70.1 0.7 fusion.10
  70.8 66.6 %all-gather.5.cloned.1.call-done = f32[16,512,256]{2,1,0:T(8,128)} async-done(((f32[2,512,256]{2,1,0:T(8,128)}), f32[16,512,256]{2,1,0:T(8,128)}) %all-gather.5.cloned.1.call-update) | async-done | bytes 8388624 | tf_op jit(solution)/shard_map/all_gather | solution.py:11
  137.5 10.8 %while.16 = (s32[]{:T(128)}, f32[2,512,256]{2,1,0:T(8,128)S(1)}, f32[2,256]{1,0:T(2,128)S(1)}, f32[2]{0:T(128)S(1)}, s32[]{:T(128)}, /*index=5*/f32[8,2]{1,0:T(8...) while((s32[]{:T(128)}, f32[2,512,256]{2,1,0:T(8,128)S(1)}, ...), condition=%wide.region_6.7_spmd, body=%wide.region_5.6_spmd.sunk | while | flops 787981 | bytes 3152135 | solution.py:19
  137.6 1.7 fusion.42
  139.4 1.7 fusion.42
  141.2 1.7 fusion.42
  143.0 1.7 fusion.42
  144.8 1.7 fusion.42
  146.6 1.7 fusion.42
  148.4 1.3 fusion.22
  149.8 2.2 %fusion.8 = bf16[512,2,512]{0,2,1:T(8,128)(2,1)S(1)} fusion(f32[2,512,512]{1,2,0:T(8,128)S(1)} %fusion.10, f32[2,512,256]{2,1,0:T(8,128)S(1)} %get-tuple-element.77, bf16[512,2,256]{0,2,1:T(8,128)(2,1)} %bitcast.119, f32[512,2]{0,1:T(2,128)S(1)} %get-tuple-element.128, f32[512,2]{0,1:T(2,128)S(1)} %get-tuple-element.130, f32[512,2]{0,1:T(2,128)S(1)} %get-tuple-element.129), kind=kOutput, calls=%fused_computation.16 | convolution fusion | flops 1613234176 | bytes 4730880 | tf_op jit(solution)/shard_map/hvk,thk->thv/dot_general | solution.py:78
  152.0 9.5 %convolution_convert_fusion = bf16[512,4096]{1,0:T(8,128)(2,1)} fusion(bf16[512,1024]{0,1:T(8,128)(2,1)S(1)} %bitcast.129, bf16[1024,4096]{1,0:T(8,128)(2,1)} %param.13), kind=kOutput, calls=%fused_computation.12 | convolution fusion | flops 4297064448 | bytes 13631488 | tf_op jit(solution)/shard_map/dot_general | solution.py:106
  162.1 45.6 %reduce-scatter.2.cloned.1.call-done = bf16[512,1024]{1,0:T(8,128)(2,1)} async-done(((bf16[512,4096]{1,0:T(8,128)(2,1)}), bf16[512,1024]{1,0:T(8,128)(2,1)}) %reduce-scatter.2.cloned.1.call-update) | async-done | bytes 1048592 | tf_op jit(solution)/shard_map/reduce_scatter | solution.py:107
  (57 shorter events, 4.4 us)
Async XLA Ops:
  7.2 3.6 %copy-start.2 = (bf16[512,512]{1,0:T(8,128)(2,1)S(1)}, bf16[512,512]{1,0:T(8,128)(2,1)}, u32[]{:S(2)}) copy-start(bf16[512,512]{1,0:T(8,128)(2,1)} %param.9) | copy-start | bytes 1572868
  7.2 3.8 %copy-start.4 = (f32[512,2]{0,1:T(2,128)S(1)}, f32[512,2]{0,1:T(2,128)}, u32[]{:S(2)}) copy-start(f32[512,2]{0,1:T(2,128)} %param.12) | copy-start | bytes 12292
  7.2 130.3 %all-gather.5.cloned.1.call-start = ((), (), s32[]{:S(2)}) async-start(), calls=%async_computation.2 | async-start | bytes 9437184 | tf_op jit(solution)/shard_map/all_gather | solution.py:11
  11.0 2.1 copy-start
  11.7 13.6 %copy-start.5 = (u32[32]{0:T(128)S(1)}, u32[32]{0:T(128)}, u32[]{:S(2)}) copy-start(u32[32]{0:T(128)} %constant.58) | copy-start | bytes 388
  13.1 194.6 %reduce-scatter.2.cloned.1.call-start = ((), (), s32[]{:S(2)}) async-start(), calls=%async_computation.1 | async-start | bytes 5242880 | tf_op jit(solution)/shard_map/reduce_scatter | solution.py:107
  43.7 25.3 %copy-start.1 = (bf16[512,512]{0,1:T(8,128)(2,1)S(1)}, bf16[512,512]{0,1:T(8,128)(2,1)}, u32[]{:S(2)}) copy-start(bf16[512,512]{0,1:T(8,128)(2,1)} %copy-done) | copy-start | bytes 1572868
  46.2 23.9 %copy-start.3 = (bf16[512,512]{0,1:T(8,128)(2,1)}, bf16[512,512]{0,1:T(8,128)(2,1)S(1)}, u32[]{:S(2)}) copy-start(bf16[512,512]{0,1:T(8,128)(2,1)S(1)} %copy.49) | copy-start | bytes 1572868
Sparse Core Ops, SparseCore 0:
  13.2 124.1 all-gather.4
  161.7 45.9 reduce-scatter.1
where the time goes:
time: 217 us; the launch traced here: 214 us
  waiting for transfers between devices  112 us (52%)
  blocking collectives  50.8 us (23%)
  matrix products  15.3 us (7%)
  other arithmetic  15 us (7%)
  between operations  14.9 us (7%)
  local copies, waits for them, and re-layouts  6.12 us (3%)
    all_gather x1, waiting for transfers between devices, entering(): gathered = jax.tree.map(lambda a: lax.all_gather(a, axis), part)  66.6 us
    reduce_scatter x1, waiting for transfers between devices, shards(): lax.psum_scatter(partial_value.astype(jnp.bfloat16), 'head', scatter_dime...  45.6 us
    all_gather x2, blocking collectives, entering(): gathered = jax.tree.map(lambda a: lax.all_gather(a, axis), part)  34.5 us
    unnamed x1, blocking collectives  16.3 us
    add x6, other arithmetic, combine_states(): e_scale[:, None, None] * e_matrix + l_scale[:, None, None] * l_matrix  10.1 us
    dot_general x1, matrix products, shards(): jnp.dot(hidden, out_weight, preferred_element_type=jnp.float32)  9.48 us
  transfers between devices with their start and end apart: 2, of which 2 were waited for; matrix products, arithmetic and copies ran while one was open for 3% of the time, Pallas kernels for 0%

commit v1 on v0

v1 whole, which is shorter than its diff:
```python
import functools

import jax
import jax.numpy as jnp
from jax import lax
from jax.experimental import pallas as pl
from jax.experimental.pallas import tpu as pltpu
from jax.sharding import PartitionSpec as P

MESH = pl.DeviceIdType.MESH
F32 = jnp.float32
BF16 = jnp.bfloat16
STATE_CHUNKS = 8
ROW_CHUNKS = 4
LOWEST = -1e30


def log_sigmoid(x):
    u = jnp.exp(-jnp.abs(x))
    s = u / (2.0 + u)
    s2 = s * s
    series = jnp.full_like(s, 1.0 / 17.0)
    for odd in (15, 13, 11, 9, 7, 5, 3, 1):
        series = series * s2 + 1.0 / odd
    return jnp.minimum(x, 0.0) - 2.0 * s * series


def kernel(
    n_seq,
    n_head,
    heads,
    dqk,
    dv,
    gates_ref,
    k_ref,
    v_ref,
    q_ref,
    w_hbm,
    out_ref,
    mean_ref,
    w_ref,
    packets,
    maxes,
    norms,
    own,
    x_in,
    fwd,
    y_in,
    carry,
    num,
    stat,
    hid,
    send_a,
    recv_a,
    send_b,
    recv_b,
    acc,
    w_sem,
    p_send,
    p_recv,
    zs_sem,
    zr_sem,
    ys_sem,
    yr_sem,
    as_sem,
    ar_sem,
    bs_sem,
    br_sem,
):
    tokens = q_ref.shape[0]
    cols = out_ref.shape[1]
    groups = n_head // 2
    me = lax.axis_index("seq")
    head = lax.axis_index("head")
    slow, fast = me // 2, lax.rem(me, 2)
    last = n_seq // 2 - 1
    group, core = head // 2, lax.rem(head, 2)

    barrier = pltpu.get_barrier_semaphore()
    for d in range(1, n_seq):
        pl.semaphore_signal(
            barrier, 1, device_id={"seq": lax.rem(me + d, n_seq)}, device_id_type=MESH
        )
    for d in range(1, n_head):
        pl.semaphore_signal(
            barrier, 1, device_id={"head": lax.rem(head + d, n_head)}, device_id_type=MESH
        )
    w_copy = pltpu.make_async_copy(w_hbm, w_ref, w_sem)
    w_copy.start()

    gates = gates_ref[...]
    pad = gates.shape[0]
    row_id = lax.broadcasted_iota(jnp.int32, (tokens, tokens), 0)
    col_id = lax.broadcasted_iota(jnp.int32, (tokens, tokens), 1)
    upper = (row_id <= col_id).astype(F32)
    causal = row_id >= col_id
    cum = jnp.dot(
        log_sigmoid(gates), upper, precision=lax.Precision.HIGHEST, preferred_element_type=F32
    )
    inp = gates[heads : 2 * heads, :]
    cum = cum[:heads, :]
    drive = inp - cum
    decay = cum[:, tokens - 1 : tokens]
    own_log = decay + drive
    own_max = jnp.max(own_log, axis=1, keepdims=True)
    key_weight = jnp.exp(own_log - own_max) * (1.0 / dqk**0.5)
    stacked = jnp.concatenate(
        [cum, key_weight, jnp.zeros((128 - 2 * heads, tokens), F32)], axis=0
    )
    columns = stacked.T

    width = packets.shape[2]
    for h in range(heads):
        kf = k_ref[:, h * dqk : (h + 1) * dqk].astype(F32)
        wk = kf * columns[:, heads + h : heads + h + 1]
        packets[me, h : h + 1, 0:dqk] = jnp.sum(wk, axis=0, keepdims=True)
        packets[me, h : h + 1, dqk:width] = jnp.zeros((1, width - dqk), F32)
        packets[me, heads + h : heads + h + 1, :] = jnp.broadcast_to(
            own_max[h : h + 1, :], (1, width)
        )
        packets[me, 2 * heads + h : 2 * heads + h + 1, :] = jnp.broadcast_to(
            decay[h : h + 1, :], (1, width)
        )
        packets[me, 3 * heads + h : 3 * heads + h + 1, :] = jnp.broadcast_to(
            jnp.sum(inp[h : h + 1, :], axis=1, keepdims=True), (1, width)
        )
        own[h * dqk : (h + 1) * dqk, :] = lax.dot_general(
            wk.astype(BF16),
            v_ref[:, h * dv : (h + 1) * dv],
            (((0,), (0,)), ((), ())),
            preferred_element_type=F32,
        ).astype(BF16)

    chunk = heads * dqk // STATE_CHUNKS

    def part(ref, c):
        return ref.at[pl.ds(c * chunk, chunk)]

    def z_copy(src, c):
        return pltpu.make_async_remote_copy(
            src_ref=part(src, c),
            dst_ref=part(x_in, c),
            send_sem=zs_sem.at[c],
            recv_sem=zr_sem.at[c],
            device_id={"seq": jnp.minimum(me + 2, n_seq - 2 + fast)},
            device_id_type=MESH,
        )

    def y_copy(src, c):
        return pltpu.make_async_remote_copy(
            src_ref=part(src, c),
            dst_ref=part(y_in, c),
            send_sem=ys_sem.at[c],
            recv_sem=yr_sem.at[c],
            device_id={"seq": me + 1 - 2 * fast},
            device_id_type=MESH,
        )

    def p_copy(d):
        return pltpu.make_async_remote_copy(
            src_ref=packets.at[me],
            dst_ref=packets.at[me],
            send_sem=p_send.at[d],
            recv_sem=p_recv.at[d],
            device_id={"seq": lax.rem(me + d, n_seq)},
            device_id_type=MESH,
        )

    pl.semaphore_wait(barrier, n_seq + n_head - 2)
    for d in range(1, n_seq):
        p_copy(d).start()
    first = slow == 0
    feeds = slow < last

    @pl.when(first)
    def _():
        for c in range(STATE_CHUNKS):
            z_copy(own, c).start()

            @pl.when(fast == 0)
            def _():
                y_copy(own, c).start()

    for h in range(heads):
        masked = jnp.where(causal, drive[h : h + 1, :], LOWEST)
        top = jnp.max(masked, axis=1, keepdims=True)
        factors = jnp.exp(masked - top)
        scores = lax.dot_general(
            q_ref[:, h * dqk : (h + 1) * dqk],
            k_ref[:, h * dqk : (h + 1) * dqk],
            (((1,), (1,)), ((), ())),
            preferred_element_type=F32,
        ) * (1.0 / dqk**0.5)
        weighted = factors * scores
        cum_col = columns[:, h : h + 1]
        stat[h] = jnp.concatenate(
            [
                jnp.broadcast_to(jnp.sum(weighted, axis=1, keepdims=True), (tokens, 128)),
                jnp.broadcast_to(top + cum_col, (tokens, 128)),
                jnp.broadcast_to(cum_col, (tokens, 128)),
            ],
            axis=1,
        )
        num[:, h * dv : (h + 1) * dv] = jnp.dot(
            weighted.astype(BF16), v_ref[:, h * dv : (h + 1) * dv], preferred_element_type=F32
        )

    for d in range(1, n_seq):
        pltpu.make_async_remote_copy(
            src_ref=packets.at[me],
            dst_ref=packets.at[lax.rem(me + n_seq - d, n_seq)],
            send_sem=p_send.at[d],
            recv_sem=p_recv.at[d],
            device_id={"seq": lax.rem(me + d, n_seq)},
            device_id_type=MESH,
        ).wait()

    big = jnp.full((heads, width), LOWEST, F32)
    nrm = jnp.zeros((heads, width), F32)
    total = jnp.zeros((heads, width), F32)
    maxes[0] = big
    norms[0] = nrm
    for i in range(n_seq):
        block = packets[i]
        m_i = block[heads : 2 * heads, :]
        g_i = block[2 * heads : 3 * heads, :]
        total = total + block[3 * heads : 4 * heads, :]
        merged = jnp.maximum(big + g_i, m_i)
        nrm = jnp.exp(big + g_i - merged) * nrm + jnp.exp(m_i - merged) * block[0:heads, :]
        big = merged
        maxes[i + 1] = big
        norms[i + 1] = nrm
    mean_ref[...] = total[:, 0:128] * (1.0 / (tokens * n_seq))

    prev = jnp.maximum(me - 1, 0)
    prev2 = jnp.maximum(me - 2, 0)
    max_me = maxes[me]
    max_next = maxes[me + 1]
    m_own = packets[me][heads : 2 * heads, :]
    g_own = packets[me][2 * heads : 3 * heads, :]
    g_prev = packets[prev][2 * heads : 3 * heads, :]
    m_prev = packets[prev][heads : 2 * heads, :]
    m_prev2 = packets[prev2][heads : 2 * heads, :]
    x_ref_max = jnp.where(slow == 1, m_prev2, maxes[prev])
    y_ref_max = jnp.where((slow == 1) & (fast == 0), m_prev, max_me)
    x_next = jnp.exp(jnp.minimum(x_ref_max + g_prev + g_own - max_next, 0.0))
    own_next = jnp.exp(m_own - max_next)
    x_here = jnp.exp(jnp.minimum(x_ref_max + g_prev - max_me, 0.0))
    y_here = jnp.exp(jnp.minimum(y_ref_max - max_me, 0.0))

    def scale(array, c):
        h = c * chunk // dqk
        return array[h : h + 1, :]

    @pl.when(slow > 0)
    def _():
        for c in range(STATE_CHUNKS):
            z_copy(x_in, c).wait_recv()

            @pl.when(fast == 1)
            def _():
                y_copy(x_in, c).start()

            @pl.when(feeds | (fast == 0))
            def _():
                rows = pl.ds(c * chunk, chunk)
                fwd[rows, :] = (
                    x_in[rows, :].astype(F32) * scale(x_next, c)
                    + own[rows, :].astype(F32) * scale(own_next, c)
                ).astype(BF16)

                @pl.when(feeds)
                def _():
                    z_copy(fwd, c).start()

                @pl.when(fast == 0)
                def _():
                    y_copy(fwd, c).start()

    @pl.when(me == 0)
    def _():
        carry[...] = jnp.zeros_like(carry)

    @pl.when(me > 0)
    def _():
        for c in range(STATE_CHUNKS):
            rows = pl.ds(c * chunk, chunk)
            y_copy(y_in, c).wait_recv()
            got = y_in[rows, :].astype(F32) * scale(y_here, c)

            @pl.when(first)
            def _():
                carry[rows, :] = got.astype(BF16)

            @pl.when(slow > 0)
            def _():
                carry[rows, :] = (got + x_in[rows, :].astype(F32) * scale(x_here, c)).astype(BF16)

    w_copy.wait()

    span = tokens // ROW_CHUNKS
    norm_me = norms[me]

    def a_copy(gg, r):
        return pltpu.make_async_remote_copy(
            src_ref=send_a.at[gg, pl.ds(r * span, span)],
            dst_ref=recv_a.at[gg, pl.ds(r * span, span)],
            send_sem=as_sem.at[gg, r],
            recv_sem=ar_sem.at[gg, r],
            device_id={"head": head + 1 - 2 * core},
            device_id_type=MESH,
        )

    def b_copy(gg, r):
        return pltpu.make_async_remote_copy(
            src_ref=send_b.at[gg - 1, pl.ds(r * span, span)],
            dst_ref=recv_b.at[gg - 1, pl.ds(r * span, span)],
            send_sem=bs_sem.at[gg - 1, r],
            recv_sem=br_sem.at[gg - 1, r],
            device_id={"head": lax.rem(group + gg, groups) * 2 + core},
            device_id_type=MESH,
        )

    def project(gg, side, r):
        place = lax.rem(group + gg, groups) * 2 + side
        return jnp.dot(
            hid[pl.ds(pl.multiple_of(r * span, span), span), :],
            w_ref[:, pl.ds(pl.multiple_of(place * cols, cols), cols)],
            preferred_element_type=F32,
        )

    def rows_of(r):
        return pl.ds(pl.multiple_of(r * span, span), span)

    def hidden(r):
        rows = rows_of(r)
        for h in range(heads):
            q = q_ref[rows, h * dqk : (h + 1) * dqk]
            carried_num = jnp.dot(
                q, carry[h * dqk : (h + 1) * dqk, :], preferred_element_type=F32
            )
            carried_den = jnp.sum(q.astype(F32) * norm_me[h : h + 1, 0:dqk], axis=1, keepdims=True)
            stats = stat[h, rows, :]
            intra_den = stats[:, 0:1]
            intra_max = stats[:, 128:129]
            carried_log = stats[:, 256:257] + max_me[h : h + 1, 0:1]
            stabilizer = jnp.maximum(intra_max, carried_log)
            a = jnp.exp(intra_max - stabilizer)
            c = jnp.exp(carried_log - stabilizer)
            den = jnp.maximum(jnp.abs(a * intra_den + c * carried_den), 1.0)
            hid[rows, h * dv : (h + 1) * dv] = (
                num[rows, h * dv : (h + 1) * dv] * (a / den) + carried_num * (c / den)
            ).astype(BF16)

    def sweep(r, _):
        @pl.when(r < ROW_CHUNKS)
        def _():
            hidden(r)
            for gg in range(1, groups):
                send_a[gg, rows_of(r), :] = project(gg, 1 - core, r).astype(BF16)
                a_copy(gg, r).start()

        @pl.when(r > 0)
        def _():
            rr = r - 1
            for gg in range(1, groups):
                mine = project(gg, core, rr)
                a_copy(gg, rr).wait_recv()
                send_b[gg - 1, rows_of(rr), :] = (
                    mine + recv_a[gg, rows_of(rr), :].astype(F32)
                ).astype(BF16)
                b_copy(gg, rr).start()

        return 0

    lax.fori_loop(0, ROW_CHUNKS + 1, sweep, 0)

    def local_a(r, _):
        send_a[0, rows_of(r), :] = project(0, 1 - core, r).astype(BF16)
        a_copy(0, r).start()
        return 0

    lax.fori_loop(0, ROW_CHUNKS, local_a, 0)

    def local_b(r, _):
        mine = project(0, core, r)
        a_copy(0, r).wait_recv()
        acc[rows_of(r), :] = mine + recv_a[0, rows_of(r), :].astype(F32)
        return 0

    lax.fori_loop(0, ROW_CHUNKS, local_b, 0)

    def finish(r, _):
        value = acc[rows_of(r), :]
        for gg in range(1, groups):
            b_copy(gg, r).wait_recv()
            value = value + recv_b[gg - 1, rows_of(r), :].astype(F32)
        out_ref[rows_of(r), :] = value.astype(out_ref.dtype)
        return 0

    lax.fori_loop(0, ROW_CHUNKS, finish, 0)

    for c in range(STATE_CHUNKS):

        @pl.when(feeds)
        def _():
            z_copy(own, c).wait_send()

        @pl.when((fast == 0) | (slow > 0))
        def _():
            y_copy(own, c).wait_send()

    for r in range(ROW_CHUNKS):
        for gg in range(groups):
            a_copy(gg, r).wait_send()
        for gg in range(1, groups):
            b_copy(gg, r).wait_send()


def shards(n_seq, n_head, queries, keys, values, forget_gate, input_gate, out_weight):
    tokens = queries.shape[0]
    heads = forget_gate.shape[1]
    dqk = queries.shape[1] // heads
    dv = values.shape[1] // heads
    cols = out_weight.shape[1] // n_head
    groups = n_head // 2
    pad = -(-2 * heads // 8) * 8
    gates = jnp.concatenate(
        [
            forget_gate.T,
            input_gate.T,
            jnp.zeros((pad - 2 * heads, tokens), F32),
        ],
        axis=0,
    )
    width = max(dqk, dv)
    state = (heads * dqk, dv)
    vmem = pl.BlockSpec(memory_space=pltpu.VMEM)
    dma = pltpu.SemaphoreType.DMA
    mixed, mean = pl.pallas_call(
        functools.partial(kernel, n_seq, n_head, heads, dqk, dv),
        out_shape=(
            jax.ShapeDtypeStruct((tokens, cols), BF16),
            jax.ShapeDtypeStruct((heads, 128), F32),
        ),
        in_specs=[vmem] * 4 + [pl.BlockSpec(memory_space=pl.ANY)],
        out_specs=(vmem, vmem),
        scratch_shapes=[
            pltpu.VMEM(out_weight.shape, BF16),
            pltpu.VMEM((n_seq, 4 * heads, width), F32),
            pltpu.VMEM((n_seq + 1, heads, width), F32),
            pltpu.VMEM((n_seq + 1, heads, width), F32),
            pltpu.VMEM(state, BF16),
            pltpu.VMEM(state, BF16),
            pltpu.VMEM(state, BF16),
            pltpu.VMEM(state, BF16),
            pltpu.VMEM(state, BF16),
            pltpu.VMEM((tokens, heads * dv), F32),
            pltpu.VMEM((heads, tokens, 384), F32),
            pltpu.VMEM((tokens, heads * dv), BF16),
            pltpu.VMEM((groups, tokens, cols), BF16),
            pltpu.VMEM((groups, tokens, cols), BF16),
            pltpu.VMEM((groups - 1, tokens, cols), BF16),
            pltpu.VMEM((groups - 1, tokens, cols), BF16),
            pltpu.VMEM((tokens, cols), F32),
            dma,
            dma((n_seq,)),
            dma((n_seq,)),
            dma((STATE_CHUNKS,)),
            dma((STATE_CHUNKS,)),
            dma((STATE_CHUNKS,)),
            dma((STATE_CHUNKS,)),
            dma((groups, ROW_CHUNKS)),
            dma((groups, ROW_CHUNKS)),
            dma((groups - 1, ROW_CHUNKS)),
            dma((groups - 1, ROW_CHUNKS)),
        ],
        compiler_params=pltpu.CompilerParams(
            collective_id=0, has_side_effects=True, vmem_limit_bytes=60 * 1024 * 1024
        ),
    )(gates, keys, values, queries, out_weight)
    return mixed, mean[:, 0]


def solution(mesh):
    placed = (
        P("seq", "head"),
        P("seq", "head"),
        P("seq", "head"),
        P("seq", "head"),
        P("seq", "head"),
        P("head", None),
    )
    return jax.shard_map(
        functools.partial(shards, mesh.shape["seq"], mesh.shape["head"]),
        mesh=mesh,
        in_specs=placed,
        out_specs=(P("seq", "head"), P("head")),
        check_vma=False,
    )
```

time: 217 us -> 64.5 us (0.30); the launches traced: 214 us -> 64.2 us
  waiting for transfers between devices: 112 us -> 0 us
  Pallas kernels: 0 us -> 58.6 us
  blocking collectives: 50.8 us -> 0 us
  matrix products: 15.3 us -> 0 us
  between operations: 14.9 us -> 0.65 us
  other arithmetic: 15 us -> 1.38 us
  local copies, waits for them, and re-layouts: 6.12 us -> 3.64 us
    all_gather x1 -> x0, waiting for transfers between devices: 66.6 us -> none  [entering(): gathered = jax.tree.map(lambda a: lax.all_gather(a, axis), part)]
    pallas_call x0 -> x1, Pallas kernels: none -> 58.6 us  [shards(): pl.pallas_call(functools.partial(kernel, n_seq, n_head, heads, dqk, dv),...]
    reduce_scatter x1 -> x0, waiting for transfers between devices: 45.6 us -> none  [shards(): lax.psum_scatter(partial_value.astype(jnp.bfloat16), 'head', scatter_dime...]
    all_gather x2 -> x0, blocking collectives: 34.5 us -> none  [entering(): gathered = jax.tree.map(lambda a: lax.all_gather(a, axis), part)]
    unnamed x1 -> x0, blocking collectives: 16.3 us -> none
    dot_general x6 -> x0, matrix products: 15.3 us -> none  [the longest x1 9.48 us: shards(): jnp.dot(hidden, out_weight, preferred_element_type=jnp.float32)]
    add x12 -> x0, other arithmetic: 10.6 us -> none  [the longest x6 10.1 us: combine_states(): e_scale[:, None, None] * e_matrix + l_scale[:, None, None] * l_matrix]
    reshape x4 -> x0, local copies, waits for them, and re-layouts: 2.98 us -> none  [the longest x1 1.5 us: shards(): v_heads = values.reshape(token_count, head_count, v_width)]
  transfers between devices with their start and end apart: 2 -> 0, of which waited for: 2 -> 0; matrix products, arithmetic and copies ran while one was open for 3% -> 0% of each run, Pallas kernels for 0% -> 0%
where the time goes in v1:
time: 64.5 us; the launch traced here: 64.2 us
  Pallas kernels  58.6 us (91%)
  local copies, waits for them, and re-layouts  3.64 us (6%)
  other arithmetic  1.38 us (2%)
  between operations  0.65 us (1%)
    pallas_call x1, Pallas kernels, shards(): pl.pallas_call(functools.partial(kernel, n_seq, n_head, heads, dqk, dv),...  58.6 us
    unnamed x1, local copies, waits for them, and re-layouts  2.26 us
    concatenate x1, other arithmetic, shards(): jnp.concatenate([forget_gate.T, input_gate.T, jnp.zeros((pad - 2 * heads,...  1.38 us
    slice x1, local copies, waits for them, and re-layouts, shards(): return (mixed, mean[:, 0])  1.3 us

profile of v1, /device:TPU:25, one launch (start us, length us, event | category | flops | bytes accessed | tf_op | source)
XLA Modules:
  0.0 64.2 jit_solution(16154001122559940755)
XLA Ops:
  0.6 0.1 pad.2.clone
  0.7 1.4 %maximum_maximum_fusion.gates_ref = f32[8,512]{1,0:T(8,128)} fusion(f32[2,512]{1,0:T(2,128)} %bitcast.2, f32[2,512]{1,0:T(2,128)} %bitcast.3, f32[8]{0:T(128)S(1)} %pad.2.clone), kind=kLoop, calls=%fused_computation | loop fusion | flops 8192 | bytes 24608 | tf_op jit(solution)/shard_map/concatenate | solution.py:428
  2.1 58.6 %shard_map.77 = (bf16[512,1024]{1,0:T(8,128)(2,1)}, f32[2,128]{1,0:T(2,128)}) custom-call(f32[8,512]{1,0:T(8,128)} %maximum_maximum_fusion.gates_ref, bf16[512,512]{1,0:T(8,128)(2,1)} %k_ref.1, bf16[512,1024]{1,0:T(8,128)(2,1)} %v_ref.1, bf16[512,512]{1,0:T(8,128)(2,1)} %q_ref.1, bf16[1024,4096]{1,0:T(8,128)(2,1)} %w_hbm.1), custom_call_target="tpu_custom_call" | custom-call | tf_op jit(solution)/shard_map/pallas_call | solution.py:440
  60.7 1.3 %slice_reduce_fusion = f32[2]{0:T(128)} fusion(f32[2,128]{1,0:T(2,128)} %get-tuple-element.5), kind=kLoop, calls=%fused_computation.1 | loop fusion | bytes 16 | tf_op jit(solution)/shard_map/slice | solution.py:482
  62.0 2.3 %copy.9 = bf16[512,1024]{1,0:T(8,128)(2,1)} copy(bf16[512,1024]{1,0:T(8,128)(2,1)} %get-tuple-element.8) | data formatting | bytes 2097152
  (1 shorter events, 0.0 us)

commit v2 on v1

--- a/solution.py
+++ b/solution.py
@@ -10,8 +10,9 @@
 MESH = pl.DeviceIdType.MESH
 F32 = jnp.float32
 BF16 = jnp.bfloat16
-STATE_CHUNKS = 8
+STATE_CHUNKS = 16
 ROW_CHUNKS = 4
+TAIL_CHUNKS = 2
 LOWEST = -1e30
 
 
@@ -31,17 +32,23 @@
     heads,
     dqk,
     dv,
-    gates_ref,
+    forget_ref,
+    input_ref,
+    k_hbm,
+    v_hbm,
+    q_hbm,
+    w_hbm,
+    acc_hbm,
+    recv_b,
+    mean_ref,
     k_ref,
     v_ref,
     q_ref,
-    w_hbm,
-    out_ref,
-    mean_ref,
     w_ref,
     packets,
     maxes,
     norms,
+    wkb,
     own,
     x_in,
     fwd,
@@ -53,8 +60,8 @@
     send_a,
     recv_a,
     send_b,
-    recv_b,
     acc,
+    in_sem,
     w_sem,
     p_send,
     p_recv,
@@ -66,9 +73,16 @@
     ar_sem,
     bs_sem,
     br_sem,
+    acc_sem,
 ):
+    loads = [
+        pltpu.make_async_copy(src, dst, in_sem.at[i])
+        for i, (src, dst) in enumerate(((k_hbm, k_ref), (v_hbm, v_ref), (q_hbm, q_ref)))
+    ]
+    for load in loads:
+        load.start()
     tokens = q_ref.shape[0]
-    cols = out_ref.shape[1]
+    cols = acc_hbm.shape[1]
     groups = n_head // 2
     me = lax.axis_index("seq")
     head = lax.axis_index("head")
@@ -88,17 +102,20 @@
     w_copy = pltpu.make_async_copy(w_hbm, w_ref, w_sem)
     w_copy.start()
 
-    gates = gates_ref[...]
-    pad = gates.shape[0]
     row_id = lax.broadcasted_iota(jnp.int32, (tokens, tokens), 0)
     col_id = lax.broadcasted_iota(jnp.int32, (tokens, tokens), 1)
-    upper = (row_id <= col_id).astype(F32)
+    upper = (row_id <= col_id).astype(F32).astype(BF16)
     causal = row_id >= col_id
-    cum = jnp.dot(
-        log_sigmoid(gates), upper, precision=lax.Precision.HIGHEST, preferred_element_type=F32
+    inp = input_ref[...]
+    log_forget = jnp.concatenate(
+        [log_sigmoid(forget_ref[...]), jnp.zeros((8 - heads % 8, tokens), F32)], axis=0
     )
-    inp = gates[heads : 2 * heads, :]
-    cum = cum[:heads, :]
+    high = log_forget.astype(BF16).astype(F32)
+    middle = (log_forget - high).astype(BF16).astype(F32)
+    pieces = jnp.concatenate([high, middle, log_forget - high - middle], axis=0)
+    sums = jnp.dot(pieces.astype(BF16), upper, preferred_element_type=F32)
+    pad = log_forget.shape[0]
+    cum = (sums[2 * pad :] + sums[pad : 2 * pad] + sums[:pad])[:heads, :]
     drive = inp - cum
     decay = cum[:, tokens - 1 : tokens]
     own_log = decay + drive
@@ -110,6 +127,7 @@
     columns = stacked.T
 
     width = packets.shape[2]
+    loads[0].wait()
     for h in range(heads):
         kf = k_ref[:, h * dqk : (h + 1) * dqk].astype(F32)
         wk = kf * columns[:, heads + h : heads + h + 1]
@@ -124,12 +142,7 @@
         packets[me, 3 * heads + h : 3 * heads + h + 1, :] = jnp.broadcast_to(
             jnp.sum(inp[h : h + 1, :], axis=1, keepdims=True), (1, width)
         )
-        own[h * dqk : (h + 1) * dqk, :] = lax.dot_general(
-            wk.astype(BF16),
-            v_ref[:, h * dv : (h + 1) * dv],
-            (((0,), (0,)), ((), ())),
-            preferred_element_type=F32,
-        ).astype(BF16)
+        wkb[:, h * dqk : (h + 1) * dqk] = wk.astype(BF16)
 
     chunk = heads * dqk // STATE_CHUNKS
 
@@ -172,15 +185,26 @@
     first = slow == 0
     feeds = slow < last
 
-    @pl.when(first)
-    def _():
-        for c in range(STATE_CHUNKS):
-            z_copy(own, c).start()
-
-            @pl.when(fast == 0)
-            def _():
-                y_copy(own, c).start()
-
+    loads[1].wait()
+    per_head = STATE_CHUNKS // heads
+    for h in range(heads):
+        own[h * dqk : (h + 1) * dqk, :] = lax.dot_general(
+            wkb[:, h * dqk : (h + 1) * dqk],
+            v_ref[:, h * dv : (h + 1) * dv],
+            (((0,), (0,)), ((), ())),
+            preferred_element_type=F32,
+        ).astype(BF16)
+
+        @pl.when(first)
+        def _():
+            for c in range(h * per_head, (h + 1) * per_head):
+                z_copy(own, c).start()
+
+                @pl.when(fast == 0)
+                def _():
+                    y_copy(own, c).start()
+
+    loads[2].wait()
     for h in range(heads):
         masked = jnp.where(causal, drive[h : h + 1, :], LOWEST)
         top = jnp.max(masked, axis=1, keepdims=True)
@@ -230,7 +254,8 @@
         big = merged
         maxes[i + 1] = big
         norms[i + 1] = nrm
-    mean_ref[...] = total[:, 0:128] * (1.0 / (tokens * n_seq))
+    for h in range(heads):
+        mean_ref[h] = total[h, 0] * (1.0 / (tokens * n_seq))
 
     prev = jnp.maximum(me - 1, 0)
     prev2 = jnp.maximum(me - 2, 0)
@@ -382,23 +407,17 @@
 
     lax.fori_loop(0, ROW_CHUNKS, local_a, 0)
 
+    def acc_copy(r):
+        return pltpu.make_async_copy(acc.at[rows_of(r)], acc_hbm.at[rows_of(r)], acc_sem.at[r])
+
     def local_b(r, _):
         mine = project(0, core, r)
         a_copy(0, r).wait_recv()
-        acc[rows_of(r), :] = mine + recv_a[0, rows_of(r), :].astype(F32)
+        acc[rows_of(r), :] = (mine + recv_a[0, rows_of(r), :].astype(F32)).astype(BF16)
+        acc_copy(r).start()
         return 0
 
     lax.fori_loop(0, ROW_CHUNKS, local_b, 0)
-
-    def finish(r, _):
-        value = acc[rows_of(r), :]
-        for gg in range(1, groups):
-            b_copy(gg, r).wait_recv()
-            value = value + recv_b[gg - 1, rows_of(r), :].astype(F32)
-        out_ref[rows_of(r), :] = value.astype(out_ref.dtype)
-        return 0
-
-    lax.fori_loop(0, ROW_CHUNKS, finish, 0)
 
     for c in range(STATE_CHUNKS):
 
@@ -411,10 +430,21 @@
             y_copy(own, c).wait_send()
 
     for r in range(ROW_CHUNKS):
+        acc_copy(r).wait()
         for gg in range(groups):
             a_copy(gg, r).wait_send()
         for gg in range(1, groups):
             b_copy(gg, r).wait_send()
+            b_copy(gg, r).wait_recv()
+
+
+def finish(acc_ref, recv_ref, mean_ref, out_ref, final_ref):
+    value = acc_ref[...].astype(F32)
+    for gg in range(recv_ref.shape[0]):
+        value = value + recv_ref[gg].astype(F32)
+    out_ref[...] = value.astype(out_ref.dtype)
+    for h in range(final_ref.shape[0]):
+        final_ref[h] = mean_ref[h]
 
 
 def shards(n_seq, n_head, queries, keys, values, forget_gate, input_gate, out_weight):
@@ -424,32 +454,30 @@
     dv = values.shape[1] // heads
     cols = out_weight.shape[1] // n_head
     groups = n_head // 2
-    pad = -(-2 * heads // 8) * 8
-    gates = jnp.concatenate(
-        [
-            forget_gate.T,
-            input_gate.T,
-            jnp.zeros((pad - 2 * heads, tokens), F32),
-        ],
-        axis=0,
-    )
     width = max(dqk, dv)
     state = (heads * dqk, dv)
     vmem = pl.BlockSpec(memory_space=pltpu.VMEM)
     dma = pltpu.SemaphoreType.DMA
-    mixed, mean = pl.pallas_call(
+    hbm = pl.BlockSpec(memory_space=pltpu.HBM)
+    smem = pl.BlockSpec(memory_space=pltpu.SMEM)
+    kept, received, mean = pl.pallas_call(
         functools.partial(kernel, n_seq, n_head, heads, dqk, dv),
         out_shape=(
             jax.ShapeDtypeStruct((tokens, cols), BF16),
-            jax.ShapeDtypeStruct((heads, 128), F32),
+            jax.ShapeDtypeStruct((groups - 1, tokens, cols), BF16),
+            jax.ShapeDtypeStruct((heads,), F32),
         ),
-        in_specs=[vmem] * 4 + [pl.BlockSpec(memory_space=pl.ANY)],
-        out_specs=(vmem, vmem),
+        in_specs=[vmem] * 2 + [hbm] * 4,
+        out_specs=(hbm, hbm, smem),
         scratch_shapes=[
+            pltpu.VMEM(keys.shape, BF16),
+            pltpu.VMEM(values.shape, BF16),
+            pltpu.VMEM(queries.shape, BF16),
             pltpu.VMEM(out_weight.shape, BF16),
             pltpu.VMEM((n_seq, 4 * heads, width), F32),
             pltpu.VMEM((n_seq + 1, heads, width), F32),
             pltpu.VMEM((n_seq + 1, heads, width), F32),
+            pltpu.VMEM((tokens, heads * dqk), BF16),
             pltpu.VMEM(state, BF16),
             pltpu.VMEM(state, BF16),
             pltpu.VMEM(state, BF16),
@@ -461,8 +489,8 @@
             pltpu.VMEM((groups, tokens, cols), BF16),
             pltpu.VMEM((groups, tokens, cols), BF16),
             pltpu.VMEM((groups - 1, tokens, cols), BF16),
-            pltpu.VMEM((groups - 1, tokens, cols), BF16),
-            pltpu.VMEM((tokens, cols), F32),
+            pltpu.VMEM((tokens, cols), BF16),
+            dma((3,)),
             dma,
             dma((n_seq,)),
             dma((n_seq,)),
@@ -474,12 +502,29 @@
             dma((groups, ROW_CHUNKS)),
             dma((groups - 1, ROW_CHUNKS)),
             dma((groups - 1, ROW_CHUNKS)),
+            dma((ROW_CHUNKS,)),
         ],
         compiler_params=pltpu.CompilerParams(
-            collective_id=0, has_side_effects=True, vmem_limit_bytes=60 * 1024 * 1024
+            collective_id=0, has_side_effects=True, vmem_limit_bytes=62 * 1024 * 1024
         ),
-    )(gates, keys, values, queries, out_weight)
-    return mixed, mean[:, 0]
+    )(forget_gate.T, input_gate.T, keys, values, queries, out_weight)
+    span = tokens // TAIL_CHUNKS
+    mixed, mean = pl.pallas_call(
+        finish,
+        grid=(TAIL_CHUNKS,),
+        out_shape=(
+            jax.ShapeDtypeStruct((tokens, cols), BF16),
+            jax.ShapeDtypeStruct((heads,), F32),
+        ),
+        in_specs=[
+            pl.BlockSpec((span, cols), lambda i: (i, 0)),
+            pl.BlockSpec((groups - 1, span, cols), lambda i: (0, i, 0)),
+            smem,
+        ],
+        out_specs=(pl.BlockSpec((span, cols), lambda i: (i, 0)), smem),
+        compiler_params=pltpu.CompilerParams(vmem_limit_bytes=62 * 1024 * 1024),
+    )(kept, received, mean)
+    return mixed, mean
 
 
 def solution(mesh):

time: 64.5 us -> 59.4 us (0.921)
  local copies, waits for them, and re-layouts: 3.64 us -> 0 us
  other arithmetic: 1.38 us -> 0 us
    pallas_call x1, Pallas kernels: 58.6 us -> 56.1 us  [shards(): pl.pallas_call(functools.partial(kernel, n_seq, n_head, heads, dqk, dv),...]
    pallas_call x0 -> x1, Pallas kernels: none -> 2.46 us  [shards(): pl.pallas_call(finish, grid=(TAIL_CHUNKS,), out_shape=(jax.ShapeDtypeStru...]
    unnamed x1 -> x0, local copies, waits for them, and re-layouts: 2.26 us -> none
    concatenate x1 -> x0, other arithmetic: 1.38 us -> none  [shards(): jnp.concatenate([forget_gate.T, input_gate.T, jnp.zeros((pad - 2 * heads,...]
    slice x1 -> x0, local copies, waits for them, and re-layouts: 1.3 us -> none  [shards(): return (mixed, mean[:, 0])]
where the time goes in v2:
time: 59.4 us; the launch traced here: 59.2 us
  Pallas kernels  58.5 us (98%)
  between operations  0.64 us (1%)
    pallas_call x1, Pallas kernels, shards(): pl.pallas_call(functools.partial(kernel, n_seq, n_head, heads, dqk, dv),...  56.1 us
    pallas_call x1, Pallas kernels, shards(): pl.pallas_call(finish, grid=(TAIL_CHUNKS,), out_shape=(jax.ShapeDtypeStru...  2.46 us

profile of v2, /device:TPU:25, one launch (start us, length us, event | category | flops | bytes accessed | tf_op | source)
XLA Modules:
  0.0 59.2 jit_solution(570132655096869149)
XLA Ops:
  0.6 56.1 %shard_map.77 = (bf16[512,1024]{1,0:T(8,128)(2,1)}, bf16[1,512,1024]{2,1,0:T(8,128)(2,1)}, f32[2]{0:T(128)}) custom-call(f32[2,512]{1,0:T(2,128)} %bitcast.2, f32[2,512]{1,0:T(2,128)} %bitcast.3, bf16[512,512]{1,0:T(8,128)(2,1)} %k_hbm.1, bf16[512,1024]{1,0:T(8,128)(2,1)} %v_hbm.1, bf16[512,512]{1,0:T(8,128)(2,1)} %q_hbm.1, bf16[1024,4096]{1,0:T(8,128)(2,1)} %w_hbm.1), custom_call_target="tpu_custom_call" | custom-call | tf_op jit(solution)/shard_map/pallas_call | solution.py:463
  56.7 2.5 %shard_map.78 = (bf16[512,1024]{1,0:T(8,128)(2,1)}, f32[2]{0:T(128)}) custom-call(bf16[512,1024]{1,0:T(8,128)(2,1)} %get-tuple-element.5.acc_ref, bf16[1,512,1024]{2,1,0:T(8,128)(2,1)} %get-tuple-element.6.recv_ref, f32[2]{0:T(128)} %get-tuple-element.7.mean_ref), custom_call_target="tpu_custom_call" | custom-call | tf_op jit(solution)/shard_map/pallas_call | solution.py:512

commit v3 on v2

--- a/solution.py
+++ b/solution.py
@@ -100,7 +100,6 @@
             barrier, 1, device_id={"head": lax.rem(head + d, n_head)}, device_id_type=MESH
         )
     w_copy = pltpu.make_async_copy(w_hbm, w_ref, w_sem)
-    w_copy.start()
 
     row_id = lax.broadcasted_iota(jnp.int32, (tokens, tokens), 0)
     col_id = lax.broadcasted_iota(jnp.int32, (tokens, tokens), 1)
@@ -186,6 +185,7 @@
     feeds = slow < last
 
     loads[1].wait()
+    w_copy.start()
     per_head = STATE_CHUNKS // heads
     for h in range(heads):
         own[h * dqk : (h + 1) * dqk, :] = lax.dot_general(

time: 59.4 us -> 59.4 us (level)
  no operation moved by 1% of the time
where the time goes in v3:
time: 59.4 us; the launch traced here: 59.2 us
  Pallas kernels  58.5 us (98%)
  between operations  0.64 us (1%)
    pallas_call x1, Pallas kernels, shards(): pl.pallas_call(functools.partial(kernel, n_seq, n_head, heads, dqk, dv),...  56.1 us
    pallas_call x1, Pallas kernels, shards(): pl.pallas_call(finish, grid=(TAIL_CHUNKS,), out_shape=(jax.ShapeDtypeStru...  2.46 us

profile of v3, /device:TPU:25, one launch (start us, length us, event | category | flops | bytes accessed | tf_op | source)
XLA Modules:
  0.0 59.2 jit_solution(1976886812275227076)
XLA Ops:
  0.6 56.1 %shard_map.77 = (bf16[512,1024]{1,0:T(8,128)(2,1)}, bf16[1,512,1024]{2,1,0:T(8,128)(2,1)}, f32[2]{0:T(128)}) custom-call(f32[2,512]{1,0:T(2,128)} %bitcast.2, f32[2,512]{1,0:T(2,128)} %bitcast.3, bf16[512,512]{1,0:T(8,128)(2,1)} %k_hbm.1, bf16[512,1024]{1,0:T(8,128)(2,1)} %v_hbm.1, bf16[512,512]{1,0:T(8,128)(2,1)} %q_hbm.1, bf16[1024,4096]{1,0:T(8,128)(2,1)} %w_hbm.1), custom_call_target="tpu_custom_call" | custom-call | tf_op jit(solution)/shard_map/pallas_call | solution.py:463
  56.7 2.5 %shard_map.78 = (bf16[512,1024]{1,0:T(8,128)(2,1)}, f32[2]{0:T(128)}) custom-call(bf16[512,1024]{1,0:T(8,128)(2,1)} %get-tuple-element.5.acc_ref, bf16[1,512,1024]{2,1,0:T(8,128)(2,1)} %get-tuple-element.6.recv_ref, f32[2]{0:T(128)} %get-tuple-element.7.mean_ref), custom_call_target="tpu_custom_call" | custom-call | tf_op jit(solution)/shard_map/pallas_call | solution.py:512
